TPU v7x, 256 devices: a whole 4x4x8 slice. The times are simulated.
256 devices in a mesh: seq: 64 (over x, z, core), tp: 4 (over y).
Axes of the slice: x: 4, y: 4, z: 8, core: 2. Of those that a mesh axis runs over, the one named last changes fastest.
Arguments:
- layer_in: bfloat16 [49152, 2048], P('seq', 'tp'), may hold values from -6 to 6
- attn_gain: float32 [2048], replicated, may hold values from 0.1 to 1.9
- qkv_weight: bfloat16 [3, 2048, 1024], P(None, None, 'tp'), may hold values from -0.125 to 0.125
- log_decay: float32 [8, 49152], P('tp', 'seq'), may hold values from -0.1 to 0
- write_rate: float32 [8, 49152], P('tp', 'seq'), may hold values from 0 to 0.9
- head_gain: float32 [128], replicated, may hold values from 0.1 to 1.9
- out_weight: bfloat16 [1024, 2048], P('tp'), may hold values from -0.1875 to 0.1875
- ffn_gain: float32 [2048], replicated, may hold values from 0.1 to 1.9
- gate_weight: bfloat16 [2048, 2560], P(None, 'tp'), may hold values from -0.125 to 0.125
- up_weight: bfloat16 [2048, 2560], P(None, 'tp'), may hold values from -0.125 to 0.125
- down_weight: bfloat16 [2560, 2048], P('tp'), may hold values from -0.125 to 0.125
Outputs:
- layer_out: bfloat16 [49152, 2048], P('seq', 'tp')
All inputs are finite; a program needn't handle non-finite values.
Results may differ from a plain program's by a relative error of at most 0.014.
Values may be sent and summed in bfloat16 or wider, within the bound.
A program may use at most 128 MiB of HBM per device.

v0:
```python
import jax
import jax.numpy as jnp
from jax import lax
from jax.sharding import Mesh
from jax.sharding import PartitionSpec as P

SEQ = ("seq_0", "seq_1", "seq_2")


norm_floor = 0.1
head_floor = 0.05
highest = lax.Precision.HIGHEST


def nothing_yet(shard, identity):
    return jax.tree.map(
        lambda a, e: jnp.broadcast_to(jnp.asarray(e, a.dtype), a.shape), shard, identity
    )


def prefix_by_axis(shard, axes, combine, identity):
    before = start = nothing_yet(shard, identity)
    subtotal = shard
    for axis in reversed(axes):
        peers, here = (lax.axis_size(axis), lax.axis_index(axis))
        pieces = jax.tree.map(
            lambda part, kind: lax.all_gather(part.astype(kind), axis),
            subtotal,
            jax.tree.map(lambda a: jnp.bfloat16 if a.dtype == jnp.float32 else a.dtype, shard),
        )
        inside, subtotal = (start, start)
        for k in range(peers):
            passed = k < here
            subtotal = combine(
                subtotal, jax.tree.map(lambda part, own: part[k].astype(own.dtype), pieces, shard)
            )
            inside = jax.tree.map(lambda new, old: jnp.where(passed, new, old), subtotal, inside)
        before = combine(inside, before)
    return before


def in_blocks(shard, dim, peers):
    before, after = (shard.shape[:dim], shard.shape[dim + 1 :])
    return jnp.moveaxis(shard.reshape(*before, peers, -1, *after), dim, 0)


def summed_on_arrival(shard, axis, dim):
    peers = lax.axis_size(axis)
    pieces = lax.all_to_all(in_blocks(shard, dim, peers), axis, 0, 0, tiled=True)
    return jnp.sum(pieces.astype(jnp.float32), axis=0)


def from_everyone(shard, axis):
    peers = lax.axis_size(axis)
    return lax.all_to_all(
        jnp.broadcast_to(shard[None], (peers, *shard.shape)), axis, 0, 0, tiled=True
    )


def of_everyone(shard, axis):
    everything = from_everyone(shard, axis)
    return jnp.sum(everything, axis=0)


def unit_rows(vectors):
    return vectors * lax.rsqrt(jnp.sum(vectors * vectors, axis=-1, keepdims=True) + 1.0)


def compose(earlier, later):
    first_map, first_shift = earlier
    second_map, second_shift = later
    joined_map = jnp.einsum("hij,hjk->hik", second_map, first_map, precision=highest)
    joined_shift = (
        jnp.einsum("hij,hjk->hik", second_map, first_shift, precision=highest) + second_shift
    )
    return (joined_map, joined_shift)


def block_terms(queries, key_rows, values, log_decay, write_rate):
    length = key_rows.shape[2]
    width = key_rows.shape[3]
    cumul = jnp.cumsum(log_decay, axis=2)
    spread = cumul[:, :, :, None] - cumul[:, :, None, :]
    row_ids = lax.broadcasted_iota(jnp.int32, (length, length), 0)
    col_ids = lax.broadcasted_iota(jnp.int32, (length, length), 1)
    inclusive = row_ids >= col_ids
    strict = row_ids > col_ids
    weight_decay = jnp.where(inclusive, jnp.exp(jnp.minimum(spread, 0.0)), 0.0)
    key_key = jnp.einsum("hcte,hcse->hcts", key_rows, key_rows, precision=highest)
    query_key = jnp.einsum("hcte,hcse->hcts", queries, key_rows, precision=highest)
    lower_part = jnp.where(strict, write_rate[:, :, :, None] * key_key * weight_decay, 0.0)
    system = lower_part + jnp.eye(length, dtype=jnp.float32)
    growth = jnp.exp(cumul)
    right_side = jnp.concatenate(
        [write_rate[:, :, :, None] * values, (write_rate * growth)[:, :, :, None] * key_rows],
        axis=3,
    )
    solved = jax.scipy.linalg.solve_triangular(system, right_side, lower=True, unit_diagonal=True)
    wy_value = solved[:, :, :, :width]
    wy_key = solved[:, :, :, width:]
    mixing = query_key * weight_decay
    keys_tail = key_rows * jnp.exp(cumul[:, :, -1:] - cumul)[:, :, :, None]
    transfer = growth[:, :, -1][:, :, None, None] * jnp.eye(width, dtype=jnp.float32) - jnp.einsum(
        "hcte,hctf->hcef", keys_tail, wy_key, precision=highest
    )
    offset = jnp.einsum("hcte,hctf->hcef", keys_tail, wy_value, precision=highest)
    local_out = jnp.einsum("hcts,hcsf->hctf", mixing, wy_value, precision=highest)
    entry_map = growth[:, :, :, None] * queries - jnp.einsum(
        "hcts,hcse->hcte", mixing, wy_key, precision=highest
    )
    return (transfer, offset, local_out, entry_map)


def advance(carried, terms):
    return (compose(carried, terms), carried)


def body(
    layer_in,
    attn_gain,
    qkv_weight,
    log_decay,
    write_rate,
    head_gain,
    out_weight,
    ffn_gain,
    gate_weight,
    up_weight,
    down_weight,
):
    length = layer_in.shape[0]
    slice_width = layer_in.shape[1]
    full_width = ffn_gain.shape[0]
    width = head_gain.shape[0]
    local_heads = qkv_weight.shape[2] // width
    span = min(64, length)
    pieces = length // span
    whole_rows = lax.all_gather(layer_in, "tp", axis=1, tiled=True).astype(jnp.float32)
    normed = (
        whole_rows
        * lax.rsqrt(jnp.mean(whole_rows * whole_rows, axis=1, keepdims=True) + norm_floor)
        * attn_gain
    ).astype(jnp.bfloat16)
    projected = jnp.einsum("ld,cde->cle", normed, qkv_weight, preferred_element_type=jnp.float32)
    projected = projected.reshape(3, length, local_heads, width).transpose(0, 2, 1, 3)
    projected = projected.reshape(3, local_heads, pieces, span, width)
    queries = unit_rows(projected[0])
    key_rows = unit_rows(projected[1])
    values = projected[2]
    transfer, offset, local_out, entry_map = block_terms(
        queries,
        key_rows,
        values,
        log_decay.reshape(local_heads, pieces, span),
        write_rate.reshape(local_heads, pieces, span),
    )
    start = (
        jnp.broadcast_to(jnp.eye(width, dtype=jnp.float32), (local_heads, width, width)),
        jnp.zeros((local_heads, width, width), jnp.float32),
    )
    device_terms, before = lax.scan(
        advance, start, (transfer.transpose(1, 0, 2, 3), offset.transpose(1, 0, 2, 3))
    )
    local_out = local_out + jnp.einsum("hcte,chef->hctf", entry_map, before[1], precision=highest)
    entry_map = jnp.einsum("hcte,chef->hctf", entry_map, before[0], precision=highest)
    local_out = local_out.reshape(local_heads, length, width)
    entry_map = entry_map.reshape(local_heads, length, width)
    prefix = prefix_by_axis(device_terms, SEQ, compose, start)
    heads_raw = local_out + jnp.einsum("hte,hef->htf", entry_map, prefix[1], precision=highest)
    heads_out = (
        heads_raw
        * lax.rsqrt(jnp.mean(heads_raw * heads_raw, axis=-1, keepdims=True) + head_floor)
        * head_gain
    )
    heads_out = (
        heads_out.transpose(1, 0, 2).reshape(length, local_heads * width).astype(jnp.bfloat16)
    )
    attn_terms = jnp.dot(heads_out, out_weight, preferred_element_type=jnp.float32)
    attn_slice = summed_on_arrival(attn_terms.astype(jnp.bfloat16), "tp", 1)
    residual = layer_in.astype(jnp.float32) + attn_slice
    squares = of_everyone(jnp.sum(residual * residual, axis=1), "tp")
    gain_slice = lax.dynamic_slice_in_dim(ffn_gain, lax.axis_index("tp") * slice_width, slice_width)
    normed_part = (
        residual * lax.rsqrt(squares / full_width + norm_floor)[:, None] * gain_slice
    ).astype(jnp.bfloat16)
    normed_mid = lax.all_gather(normed_part, "tp", axis=1, tiled=True)
    gate_act = jnp.dot(normed_mid, gate_weight, preferred_element_type=jnp.float32)
    up_act = jnp.dot(normed_mid, up_weight, preferred_element_type=jnp.float32)
    hidden = (jax.nn.silu(gate_act) * up_act).astype(jnp.bfloat16)
    ffn_terms = jnp.dot(hidden, down_weight, preferred_element_type=jnp.float32)
    ffn_slice = summed_on_arrival(ffn_terms.astype(jnp.bfloat16), "tp", 1)
    return (residual + ffn_slice).astype(jnp.bfloat16)


def solution(mesh):
    torus = Mesh(mesh.devices.reshape(4, 8, 2, mesh.shape["tp"]), ("seq_0", "seq_1", "seq_2", "tp"))
    in_specs = (
        P(SEQ, "tp"),
        P(),
        P(None, None, "tp"),
        P("tp", SEQ),
        P("tp", SEQ),
        P(),
        P("tp", None),
        P(),
        P(None, "tp"),
        P(None, "tp"),
        P("tp", None),
    )
    out_specs = P(SEQ, "tp")
    return jax.shard_map(body, mesh=torus, in_specs=in_specs, out_specs=out_specs, check_vma=False)
```

profile of v0, /device:TPU:8, one launch (start us, length us, event | category | flops | bytes accessed | tf_op | source)
XLA Modules:
  0.0 474.5 jit_solution(16160280800578878604)
XLA Ops:
  10.0 43.3 %all-gather.9.cloned.1.call-done = bf16[768,2048]{1,0:T(8,128)(2,1)} async-done(((bf16[768,512]{1,0:T(8,128)(2,1)}), bf16[768,2048]{1,0:T(8,128)(2,1)}) %all-gather.9.cloned.1.call-update) | async-done | bytes 3145744 | tf_op jit(solution)/shard_map/all_gather | solution.py:138
  53.3 2.7 fusion.11
  56.2 3.1 fusion.15
  64.7 118.8 %custom-call.4 = f32[2,12,1,64,64]{3,4,2,1,0:T(8,128)} custom-call(f32[2,12,1,64,64]{4,3,2,1,0:T(8,128)S(1)} %fusion.28), custom_call_target="InvertDiagBlocksLowerTriangular" | custom-call | tf_op jit(solution)/shard_map/jit(_solve_triangular)/vmap(vmap())/triangular_solve | solution.py:98
  186.8 1.8 fusion.35
  189.7 4.3 convolution_bitcast_fusion
  194.0 3.2 bitcast_subtract_fusion
  197.2 27.1 %while.17 = (s32[]{:T(128)}, f32[2,128,128]{2,1,0:T(8,128)S(1)}, f32[2,128,128]{2,1,0:T(8,128)S(1)}, f32[12,2,128,128]{3,2,0,1:T(8,128)}, f32[12,2,128,128]{3,2,...) while((s32[]{:T(128)}, f32[2,128,128]{2,1,0:T(8,128)S(1)}, ...), condition=%wide.region_5.6_spmd.clone, body=%wide.region_4.5_spmd.clone.sunk | while | flops 100761600 | bytes 1967735 | solution.py:161
  224.3 3.1 convolution_add_fusion.2
  227.7 2.9 fusion.120
  230.7 1.9 all-gather
  233.0 27.0 %all-gather.1 = bf16[16,128,128]{2,1,0:T(8,128)(2,1)S(1)} all-gather(bf16[2,128,128]{2,1,0:T(8,128)(2,1)S(1)} %get-tuple-element.132), channel_id=3, replica_groups=mesh['seq_0'=4,'seq_1'=8,'seq_2'=2,'tp'=4] {'seq_1'}, dimensions={0}, use_global_device_ids=true | all-gather | bytes 589824 | tf_op jit(solution)/shard_map/all_gather | solution.py:27
  261.8 12.6 %all-gather.2 = bf16[8,128,128]{2,1,0:T(8,128)(2,1)S(1)} all-gather(bf16[2,128,128]{2,1,0:T(8,128)(2,1)S(1)} %get-tuple-element.134), channel_id=4, replica_groups=mesh['seq_0'=4,'seq_1'=8,'seq_2'=2,'tp'=4] {'seq_0'}, dimensions={0}, use_global_device_ids=true | all-gather | bytes 327680 | tf_op jit(solution)/shard_map/all_gather | solution.py:27
  274.3 1.9 all-gather.3
  276.7 25.3 %all-gather.4 = bf16[16,128,128]{2,1,0:T(8,128)(2,1)S(1)} all-gather(bf16[2,128,128]{2,1,0:T(8,128)(2,1)S(1)} %get-tuple-element.136), channel_id=6, replica_groups=mesh['seq_0'=4,'seq_1'=8,'seq_2'=2,'tp'=4] {'seq_1'}, dimensions={0}, use_global_device_ids=true | all-gather | bytes 589824 | tf_op jit(solution)/shard_map/all_gather | solution.py:27
  303.7 12.3 %all-gather.5 = bf16[8,128,128]{2,1,0:T(8,128)(2,1)S(1)} all-gather(bf16[2,128,128]{2,1,0:T(8,128)(2,1)S(1)} %get-tuple-element.138), channel_id=7, replica_groups=mesh['seq_0'=4,'seq_1'=8,'seq_2'=2,'tp'=4] {'seq_0'}, dimensions={0}, use_global_device_ids=true | all-gather | bytes 327680 | tf_op jit(solution)/shard_map/all_gather | solution.py:27
  320.9 31.9 %all_to_all.16 = bf16[4,768,512]{2,1,0:T(8,128)(2,1)S(1)} all-to-all(bf16[4,768,512]{2,1,0:T(8,128)(2,1)S(1)} %bitcast.139), channel_id=1, replica_groups=mesh['seq_0'=4,'seq_1'=8,'seq_2'=2,'tp'=4] {'tp'}, dimensions={0} | all-to-all | bytes 6291456 | tf_op jit(solution)/shard_map/all_to_all | solution.py:49
  355.1 4.7 all-to-all-start.1
  360.8 2.9 all-to-all-done.1
  364.9 39.6 %all-gather.11.cloned.1.call-done = bf16[768,2048]{1,0:T(8,128)(2,1)} async-done(((bf16[768,512]{1,0:T(8,128)(2,1)}), bf16[768,2048]{1,0:T(8,128)(2,1)}) %all-gather.11.cloned.1.call-update) | async-done | bytes 3145744 | tf_op jit(solution)/shard_map/all_gather | solution.py:186
  404.5 6.7 %fusion.122 = f32[768,640]{1,0:T(8,128)} fusion(bf16[768,2048]{1,0:T(8,128)(2,1)} %all-gather.11.cloned.1.call-done, bf16[2048,640]{1,0:T(8,128)(2,1)} %param.21), kind=kOutput, calls=%fused_computation.182 | convolution fusion | flops 2013265920 | bytes 7733248 | tf_op jit(solution)/shard_map/dot_general | solution.py:187
  411.2 10.6 %convolution_convert_fusion = bf16[768,2048]{1,0:T(8,128)(2,1)} fusion(bf16[640,2048]{1,0:T(8,128)(2,1)} %param.23, f32[768,640]{1,0:T(8,128)} %fusion.122, bf16[768,2048]{1,0:T(8,128)(2,1)S(1)} %copy-done.12, bf16[2048,640]{1,0:T(8,128)(2,1)} %param.22), kind=kOutput, calls=%fused_computation.21 | convolution fusion | flops 4031053824 | bytes 13500416 | tf_op jit(solution)/shard_map/dot_general | solution.py:190
  421.8 2.2 copy.95
  423.9 40.3 %all_to_all.17 = bf16[4,768,512]{2,1,0:T(8,128)(2,1)S(1)} all-to-all(bf16[4,768,512]{2,1,0:T(8,128)(2,1)S(1)} %bitcast.140), channel_id=1, replica_groups=mesh['seq_0'=4,'seq_1'=8,'seq_2'=2,'tp'=4] {'tp'}, dimensions={0} | all-to-all | bytes 6291456 | tf_op jit(solution)/shard_map/all_to_all | solution.py:49
  (167 shorter events, 56.2 us)
Async XLA Ops:
  6.5 49.5 %copy-start = (bf16[3,2048,256]{2,1,0:T(8,128)(2,1)S(1)}, bf16[3,2048,256]{2,1,0:T(8,128)(2,1)}, u32[]{:S(2)}) copy-start(bf16[3,2048,256]{2,1,0:T(8,128)(2,1)} %param.15) | copy-start | bytes 9437188
  6.5 46.8 %all-gather.9.cloned.1.call-start = ((), (), s32[]{:S(2)}) async-start(), calls=%async_computation.3 | async-start | bytes 3932160 | tf_op jit(solution)/shard_map/all_gather | solution.py:138
  7.3 48.8 %copy-start.13 = (f32[2048]{0:T(1024)S(1)}, f32[2048]{0:T(1024)}, u32[]{:S(2)}) copy-start(f32[2048]{0:T(1024)} %param.14) | copy-start | bytes 24580
  53.3 2.8 copy-start.6
  64.7 120.5 %copy-start.7 = (f32[2,12,64,128]{3,2,1,0:T(8,128)S(1)}, f32[2,12,64,128]{3,2,1,0:T(8,128)}, u32[]{:S(2)}) copy-start(f32[2,12,64,128]{3,2,1,0:T(8,128)} %broadcast_multiply_fusion) | copy-start | bytes 2359300
  183.5 1.7 copy-start.8
  183.5 1.7 copy-start.10
  317.8 1.5 copy-start.11
  318.3 1.2 copy-start.9
  352.8 1.1 copy-start.4
  353.9 10.9 %copy-start.2 = (f32[768,512]{1,0:T(8,128)}, f32[768,512]{1,0:T(8,128)S(1)}, u32[]{:S(2)}) copy-start(f32[768,512]{1,0:T(8,128)S(1)} %convert_reduce_fusion.1) | copy-start | bytes 4718596
  355.1 8.6 %all-to-all-start.1 = ((f32[4,1,768]{2,1,0:T(1,128)}), f32[4,1,768]{2,1,0:T(1,128)S(1)}, u32[]{:S(2)}, u32[]{:S(2)}) async-start(f32[4,1,768]{2,1,0:T(1,128)} %broadcast_in_dim.60), calls=%async_computation.1 | async-start | bytes 24576 | tf_op jit(solution)/shard_map/all_to_all | solution.py:55
  359.8 44.7 %all-gather.11.cloned.1.call-start = ((), (), s32[]{:S(2)}) async-start(), calls=%async_computation.4 | async-start | bytes 3932160 | tf_op jit(solution)/shard_map/all_gather | solution.py:186
  404.5 6.7 %copy-start.12 = (bf16[768,2048]{1,0:T(8,128)(2,1)S(1)}, bf16[768,2048]{1,0:T(8,128)(2,1)}, u32[]{:S(2)}) copy-start(bf16[768,2048]{1,0:T(8,128)(2,1)} %all-gather.11.cloned.1.call-done) | copy-start | bytes 9437188
  464.2 1.4 copy-start.3
  464.2 1.6 copy-start.5
  464.2 3.0 copy-start.1
Sparse Core Ops, SparseCore 0:
  9.1 44.1 all-gather.8
  365.0 39.4 all-gather.10
where the time goes:
time: 482 us; the launch traced here: 474 us
  blocking collectives  153 us (32%)
  other arithmetic  138 us (29%)
  waiting for transfers between devices  86.5 us (18%)
  matrix products  67.3 us (14%)
  between operations  14.5 us (3%)
  local copies, waits for them, and re-layouts  9.61 us (2%)
  starting transfers between devices  4.93 us (1%)
    another operation x3, other arithmetic, block_terms(): jax.scipy.linalg.solve_triangular(system, right_side, lower=True, unit_di...  119 us
    all_gather x6, blocking collectives, prefix_by_axis(): lax.all_gather(part.astype(kind), axis)  81 us
    all_to_all x2, blocking collectives, summed_on_arrival(): lax.all_to_all(in_blocks(shard, dim, peers), axis, 0, 0, tiled=True)  72.2 us
    all_gather x1, waiting for transfers between devices, body(): lax.all_gather(layer_in, 'tp', axis=1, tiled=True).astype(jnp.float32)  43.3 us
    all_gather x1, waiting for transfers between devices, body(): normed_mid = lax.all_gather(normed_part, 'tp', axis=1, tiled=True)  39.6 us
    dot_general x29, matrix products, compose(): jnp.einsum('hij,hjk->hik', second_map, first_shift, precision=highest)  17.9 us
    dot_general x1, matrix products, body(): ffn_terms = jnp.dot(hidden, down_weight, preferred_element_type=jnp.float32)  10.6 us
  transfers between devices with their start and end apart: 3, of which 3 were waited for; matrix products, arithmetic and copies ran while one was open for 1% of the time, Pallas kernels for 0%

commit v1 on v0

v1 whole, which is shorter than its diff:
```python
import functools

import jax
import jax.numpy as jnp
from jax import lax
from jax.experimental import pallas as pl
from jax.experimental.pallas import tpu as pltpu
from jax.sharding import Mesh
from jax.sharding import PartitionSpec as P

SEQ = ("seq_0", "seq_1", "seq_2")
MESH = pl.DeviceIdType.MESH
BF16 = jnp.bfloat16
F32 = jnp.float32

norm_floor = 0.1
head_floor = 0.05
SPAN = 128
BASE = 8


def mm(a, b, dims=((1,), (0,))):
    return lax.dot_general(
        a.astype(BF16), b.astype(BF16), (dims, ((), ())), preferred_element_type=F32
    )


def mm_exact(a, b):
    return lax.dot_general(
        a, b, (((1,), (0,)), ((), ())), preferred_element_type=F32, precision=lax.Precision.HIGHEST
    )


def mm_split(a, b):
    a_high, b_high = (a.astype(BF16), b.astype(BF16))
    a_low = (a - a_high.astype(F32)).astype(BF16)
    b_low = (b - b_high.astype(F32)).astype(BF16)
    return mm(a_high, b_high) + (mm(a_high, b_low) + mm(a_low, b_high))


def unit_rows(vectors):
    return vectors * lax.rsqrt(jnp.sum(vectors * vectors, axis=-1, keepdims=True) + 1.0)


def iotas(size):
    rows = lax.broadcasted_iota(jnp.int32, (size, size), 0)
    cols = lax.broadcasted_iota(jnp.int32, (size, size), 1)
    return (rows, cols)


def inverses(lowers):
    size = lowers[0].shape[0]
    rows, cols = iotas(size)
    same = rows // BASE == cols // BASE
    powers = [jnp.where(same, a, 0.0) for a in lowers]
    found = [jnp.where(rows == cols, 1.0, 0.0) - p for p in powers]
    reach = 2
    while reach < BASE:
        powers = [mm_split(p, p) for p in powers]
        found = [x + mm_split(x, p) for x, p in zip(found, powers)]
        reach *= 2
    block = BASE
    while block < size:
        pick = (rows // (2 * block) == cols // (2 * block)) & (rows // block != cols // block)
        inner = [mm(jnp.where(pick, a, 0.0), x) for a, x in zip(lowers, found)]
        found = [x - mm(x, y) for x, y in zip(found, inner)]
        block *= 2
    return found


def compose(earlier, later):
    first_growth, first = earlier
    second_growth, second = later
    width = first.shape[0]
    second_map = second[:, :width]
    both_growth = jnp.concatenate([second_growth, second_growth], axis=1)
    own = jnp.concatenate([first_growth * second_map, second[:, width:]], axis=1)
    return (first_growth * second_growth, both_growth * first + own - mm(second_map, first))


def apply_terms(terms, state):
    growth, both = terms
    width = both.shape[0]
    return growth * state - mm(both[:, :width], state) + both[:, width:]


def packed(terms):
    growth, both = terms
    high = growth.astype(BF16).astype(F32)
    middle = (growth - high).astype(BF16).astype(F32)
    low = growth - high - middle
    width = both.shape[0]
    row = lax.broadcasted_iota(jnp.int32, (16, width), 0)
    parts = jnp.where(row == 0, high, jnp.where(row == 1, middle, jnp.where(row == 2, low, 0.0)))
    return jnp.concatenate([both, jnp.concatenate([parts, parts], axis=1)], axis=0).astype(BF16)


def unpacked(message):
    whole = message.astype(F32)
    width = whole.shape[1] // 2
    growth = whole[width : width + 1, :width]
    growth = growth + whole[width + 1 : width + 2, :width] + whole[width + 2 : width + 3, :width]
    return (growth, whole[:width])


def choose(first, terms, others):
    return tuple(jnp.where(first, a, b) for a, b in zip(terms, others))


def ring_gather(axis, size, held, send_sem, recv_sem, between):
    here = lax.axis_index(axis)
    right, left = (lax.rem(here + 1, size), lax.rem(here + size - 1, size))

    def copy(way, step):
        owner = lax.rem(here + size - step, size) if way == 0 else lax.rem(here + step, size)
        return pltpu.make_async_remote_copy(
            src_ref=held.at[owner],
            dst_ref=held.at[owner],
            send_sem=send_sem.at[way, step],
            recv_sem=recv_sem.at[way, step],
            device_id={axis: right if way == 0 else left},
            device_id_type=MESH,
        )

    steps = (size // 2, (size - 1) // 2)
    copies = [[copy(way, step) for step in range(steps[way])] for way in (0, 1)]
    for way in (0, 1):
        if steps[way]:
            copies[way][0].start()
    for step in range(steps[0]):
        between(step)
        for way in (0, 1):
            if step < steps[way]:
                copies[way][step].wait_recv()
                if step + 1 < steps[way]:
                    copies[way][step + 1].start()
    for way in (0, 1):
        for one in copies[way]:
            one.wait_send()


def layer_kernel(
    sizes,
    x_ref,
    attn_gain_ref,
    decay_ref,
    rate_ref,
    head_gain_ref,
    ffn_gain_ref,
    qkv_hbm,
    out_hbm,
    gate_hbm,
    up_hbm,
    down_hbm,
    o_ref,
    qkv_w,
    out_w,
    gate_w,
    up_w,
    down_w,
    rows_all,
    heads_all,
    local_out,
    entry_map,
    running,
    growth_now,
    pair_mine,
    pair_other,
    z_held,
    x_held,
    picked,
    picked_growth,
    states,
    parts,
    passing,
    joined,
    landed,
    resid,
    kept,
    load_sem,
    x_send,
    x_recv,
    h_send,
    h_recv,
    r_send,
    r_recv,
    w_send,
    w_recv,
    pair_send,
    pair_recv,
    z_send,
    z_recv,
    s_send,
    s_recv,
):
    x_size, z_size, tp_size, blocks = sizes
    me = lax.axis_index("tp")
    core = lax.axis_index("seq_2")
    z_here = lax.axis_index("seq_1")
    x_here = lax.axis_index("seq_0")
    right, left = (lax.rem(me + 1, tp_size), lax.rem(me + tp_size - 1, tp_size))
    opposite = lax.rem(me + 2, tp_size)
    width = head_gain_ref.shape[1]
    heads = local_out.shape[0]
    slice_width = x_ref.shape[1]
    shard_rows = heads * width
    half = SPAN // 2
    near = {"tp": right}, {"tp": left}

    loads = [
        pltpu.make_async_copy(qkv_hbm, qkv_w, load_sem.at[0]),
        pltpu.make_async_copy(out_hbm, out_w.at[pl.ds(me * shard_rows, shard_rows)], load_sem.at[1]),
        pltpu.make_async_copy(gate_hbm, gate_w, load_sem.at[2]),
        pltpu.make_async_copy(up_hbm, up_w, load_sem.at[3]),
        pltpu.make_async_copy(down_hbm, down_w, load_sem.at[4]),
    ]
    for load in loads:
        load.start()

    barrier = pltpu.get_barrier_semaphore()
    friends = [{"tp": right}, {"tp": left}, {"seq_2": 1 - core}]
    for axis, here, size in (("seq_1", z_here, z_size), ("seq_0", x_here, x_size)):
        friends.append({axis: lax.rem(here + 1, size)})
        friends.append({axis: lax.rem(here + size - 1, size)})
    for friend in friends:
        pl.semaphore_signal(barrier, inc=1, device_id=friend, device_id_type=MESH)
    pl.semaphore_wait(barrier, len(friends))

    def span_of(block, start=0, size=SPAN):
        return pl.ds(pl.multiple_of(block * SPAN + start, half), size)

    def remote(source, target, send, recv, device):
        return pltpu.make_async_remote_copy(
            src_ref=source,
            dst_ref=target,
            send_sem=send,
            recv_sem=recv,
            device_id=device,
            device_id_type=MESH,
        )

    def x_first(block, way):
        there = rows_all.at[me, span_of(block)]
        return remote(
            x_ref.at[span_of(block)], there, x_send.at[way, block], x_recv.at[way, block], near[way]
        )

    def x_second(block, way):
        owner = left if way == 0 else right
        there = rows_all.at[owner, span_of(block, way * half, half)]
        return remote(
            there, there, x_send.at[2 + way, block], x_recv.at[2 + way, block], near[way]
        )

    def h_first(block, way):
        there = heads_all.at[me, span_of(block)]
        return remote(there, there, h_send.at[way, block], h_recv.at[way, block], near[way])

    def h_second(block, way):
        owner = left if way == 0 else right
        there = heads_all.at[owner, span_of(block, way * half, half)]
        return remote(
            there, there, h_send.at[2 + way, block], h_recv.at[2 + way, block], near[way]
        )

    def project(block):
        spread = [rows_all[j, span_of(block), :].astype(F32) for j in range(tp_size)]
        squares = sum(jnp.sum(part * part, axis=1, keepdims=True) for part in spread)
        scale = lax.rsqrt(squares * (1.0 / (tp_size * slice_width)) + norm_floor)
        normed = jnp.concatenate(
            [
                (part * scale * attn_gain_ref[:, j * slice_width : (j + 1) * slice_width]).astype(
                    BF16
                )
                for j, part in enumerate(spread)
            ],
            axis=1,
        )
        return [
            jnp.dot(normed, qkv_w[i], preferred_element_type=F32) for i in range(3)
        ]

    def recur(block):
        projected = project(block)
        rows, cols = iotas(SPAN)
        ones = jnp.ones((SPAN, SPAN), F32)
        upper = jnp.where(rows <= cols, 1.0, 0.0)
        cut = [[part[:, h * width : (h + 1) * width] for h in range(heads)] for part in projected]
        queries = [unit_rows(part) for part in cut[0]]
        keys = [unit_rows(part) for part in cut[1]]
        values = cut[2]
        decay = [decay_ref[h * blocks + block] for h in range(heads)]
        rate = [rate_ref[h * blocks + block] for h in range(heads)]
        along = [mm_exact(d, upper)[0:1] for d in decay]
        total = [mm_exact(d, ones)[0:1] for d in decay]
        down = [mm_exact(jnp.where(rows >= cols, d[0:1], 0.0), ones) for d in decay]
        beta = [mm_exact(jnp.where(rows == cols, r[0:1], 0.0), ones) for r in rate]
        fade = [
            jnp.where(rows >= cols, jnp.exp(jnp.minimum(d - a, 0.0)), 0.0)
            for d, a in zip(down, along)
        ]
        key_key = [mm(k, k, ((1,), (1,))) for k in keys]
        query_key = [mm(q, k, ((1,), (1,))) for q, k in zip(queries, keys)]
        lowers = [
            jnp.where(rows > cols, b * kk * f, 0.0) for b, kk, f in zip(beta, key_key, fade)
        ]
        inverse = inverses(lowers)
        grown = [jnp.exp(d) for d in down]
        sides = [
            jnp.concatenate([(b * g) * k, b * v], axis=1)
            for b, g, k, v in zip(beta, grown, keys, values)
        ]
        solved = [mm(x, s) for x, s in zip(inverse, sides)]
        tails = [k * jnp.exp(t - d) for k, t, d in zip(keys, total, down)]
        terms = [
            (jnp.exp(t), mm(k, s, ((0,), (0,)))) for t, k, s in zip(total, tails, solved)
        ]
        mixed = [mm(qk * f, s) for qk, f, s in zip(query_key, fade, solved)]
        for h in range(heads):
            entry = grown[h] * queries[h] - mixed[h][:, :width]
            growth = growth_now[h][0:1]
            before = running[h]
            reached = mm(entry, before)
            local_out[h, span_of(block), :] = mixed[h][:, width:] + reached[:, width:]
            entry_map[h, span_of(block), :] = (growth * entry - reached[:, :width]).astype(BF16)
            new_growth, new_terms = compose((growth, before), terms[h])
            running[h] = new_terms
            growth_now[h] = jnp.broadcast_to(new_growth, growth_now.shape[1:])

    rows_all[me] = x_ref[...]
    running[...] = jnp.zeros_like(running)
    growth_now[...] = jnp.ones_like(growth_now)
    for block in range(min(2, blocks)):
        for way in (0, 1):
            x_first(block, way).start()
    loads[0].wait()

    @pl.loop(0, blocks + 1)
    def _(block):
        @pl.when(block < blocks)
        def _():
            for way in (0, 1):
                x_first(block, way).wait_recv()
                x_second(block, way).start()

        @pl.when(block + 2 < blocks)
        def _():
            for way in (0, 1):
                x_first(block + 2, way).start()

        @pl.when(block > 0)
        def _():
            for way in (0, 1):
                x_second(block - 1, way).wait_recv()
            recur(block - 1)

    part_rows = shard_rows // 2

    def w_piece(owner, start, size):
        first = pl.multiple_of(owner * shard_rows + core * part_rows + start, part_rows // 2)
        return out_w.at[pl.ds(first, size)]

    def w_copy(index, piece, device):
        return remote(piece, piece, w_send.at[index], w_recv.at[index], device)

    partner = {"seq_2": 1 - core}
    w_first = [w_copy(way, w_piece(me, 0, part_rows), near[way]) for way in (0, 1)]
    w_second = [
        w_copy(2, w_piece(left, 0, part_rows // 2), near[0]),
        w_copy(3, w_piece(right, part_rows // 2, part_rows // 2), near[1]),
    ]
    w_across = [
        w_copy(4 + n, w_piece(owner, 0, part_rows), partner)
        for n, owner in enumerate((left, right, opposite))
    ]
    loads[1].wait()
    for one in w_first:
        one.start()

    for h in range(heads):
        pair_mine[h] = packed((growth_now[h][0:1], running[h]))
    pair_copy = remote(pair_mine, pair_other, pair_send.at[0], pair_recv.at[0], partner)
    pair_copy.start()
    pair_copy.wait_recv()
    own, other = (unpacked(pair_mine[core]), unpacked(pair_other[core]))
    z_held[z_here] = packed(compose(choose(core == 0, own, other), choose(core == 0, other, own)))

    def idle(step):
        pass

    ring_gather("seq_1", z_size, z_held, z_send, z_recv, idle)

    running_now = (jnp.ones((1, width), F32), jnp.zeros((width, 2 * width), F32))
    for j in range(z_size):

        @pl.when(z_here == j)
        def _(now=running_now):
            picked_growth[...] = jnp.broadcast_to(now[0], picked_growth.shape)
            picked[...] = now[1]

        running_now = compose(running_now, unpacked(z_held[j]))
    x_held[x_here] = packed(running_now)
    for one in w_first:
        one.wait_recv()
    for one in w_second:
        one.start()
    for one in w_across[:2]:
        one.start()
    ring_gather("seq_0", x_size, x_held, s_send, s_recv, idle)
    state = jnp.zeros((width, width), F32)
    chosen = state
    for j in range(x_size):
        chosen = jnp.where(x_here == j, state, chosen)
        if j + 1 < x_size:
            state = apply_terms(unpacked(x_held[j]), state)
    states[core] = apply_terms((picked_growth[0:1], picked[...]), chosen)
    state_copy = remote(
        states.at[core], states.at[core], pair_send.at[1], pair_recv.at[1], partner
    )
    state_copy.start()
    for one in w_second:
        one.wait_recv()
    w_across[2].start()
    state_in = remote(
        states.at[1 - core], states.at[1 - core], pair_send.at[1], pair_recv.at[1], partner
    )
    state_in.wait_recv()
    starts = [
        jnp.where(core == 0, states[h], apply_terms(unpacked(pair_other[h]), states[h])).astype(
            BF16
        )
        for h in range(heads)
    ]

    for block in range(blocks):
        outs = []
        for h in range(heads):
            raw = local_out[h, span_of(block), :] + mm(entry_map[h, span_of(block), :], starts[h])
            level = jnp.mean(raw * raw, axis=-1, keepdims=True)
            outs.append((raw * lax.rsqrt(level + head_floor) * head_gain_ref[...]).astype(BF16))
        heads_all[me, span_of(block), :] = jnp.concatenate(outs, axis=1)
        if block < 2:
            for way in (0, 1):
                h_first(block, way).start()

    for one in w_across:
        one.wait_recv()
    for load in loads[2:]:
        load.wait()

    def r_far(block, way):
        return remote(
            parts.at[block, opposite, pl.ds(way * half, half)],
            passing.at[way, block],
            r_send.at[way, block],
            r_recv.at[way, block],
            near[way],
        )

    def r_direct(block, way):
        target = right if way == 0 else left
        piece = pl.ds((1 - way) * half, half)
        return remote(
            parts.at[block, target, piece],
            landed.at[way, block, piece],
            r_send.at[2 + way, block],
            r_recv.at[2 + way, block],
            near[way],
        )

    def r_joined(block, way):
        return remote(
            joined.at[way, block],
            landed.at[way, block, pl.ds(way * half, half)],
            r_send.at[4 + way, block],
            r_recv.at[4 + way, block],
            near[way],
        )

    def feed_forward(block):
        attended = jnp.concatenate(
            [heads_all[j, span_of(block), :] for j in range(tp_size)], axis=1
        )
        squares = jnp.zeros((SPAN, 1), F32)
        for j in range(tp_size):
            piece = rows_all[j, span_of(block), :].astype(F32) + jnp.dot(
                attended,
                out_w[:, j * slice_width : (j + 1) * slice_width],
                preferred_element_type=F32,
            )
            resid[j] = piece
            squares = squares + jnp.sum(piece * piece, axis=1, keepdims=True)
        scale = lax.rsqrt(squares * (1.0 / (tp_size * slice_width)) + norm_floor)
        normed = jnp.concatenate(
            [
                (
                    resid[j] * scale * ffn_gain_ref[:, j * slice_width : (j + 1) * slice_width]
                ).astype(BF16)
                for j in range(tp_size)
            ],
            axis=1,
        )
        kept[span_of(block), :] = resid[me]
        gate_act = jnp.dot(normed, gate_w[...], preferred_element_type=F32)
        up_act = jnp.dot(normed, up_w[...], preferred_element_type=F32)
        hidden = (jax.nn.silu(gate_act) * up_act).astype(BF16)
        for j in range(tp_size):
            parts[block, j] = jnp.dot(
                hidden,
                down_w[:, j * slice_width : (j + 1) * slice_width],
                preferred_element_type=F32,
            ).astype(BF16)

    def join(block):
        for way in (0, 1):
            r_far(block, way).wait_recv()
            target = right if way == 0 else left
            joined[way, block] = (
                passing[way, block].astype(F32)
                + parts[block, target, pl.ds(way * half, half), :].astype(F32)
            ).astype(BF16)
            r_joined(block, way).start()

    def finish(block):
        for way in (0, 1):
            r_direct(block, way).wait_recv()
            r_joined(block, way).wait_recv()
        total = kept[span_of(block), :] + parts[block, me].astype(F32)
        total = total + landed[0, block].astype(F32) + landed[1, block].astype(F32)
        o_ref[span_of(block), :] = total.astype(BF16)

    @pl.loop(0, blocks + 3)
    def _(block):
        @pl.when(block < blocks)
        def _():
            for way in (0, 1):
                h_first(block, way).wait_recv()
                h_second(block, way).start()

        @pl.when(block + 2 < blocks)
        def _():
            for way in (0, 1):
                h_first(block + 2, way).start()

        @pl.when((block > 1) & (block < blocks + 2))
        def _():
            join(block - 2)

        @pl.when((block > 0) & (block < blocks + 1))
        def _():
            for way in (0, 1):
                h_second(block - 1, way).wait_recv()
            feed_forward(block - 1)
            for way in (0, 1):
                r_far(block - 1, way).start()
                r_direct(block - 1, way).start()

        @pl.when(block > 2)
        def _():
            finish(block - 3)

    @pl.loop(0, blocks)
    def _(block):
        for way in (0, 1):
            x_first(block, way).wait_send()
            x_second(block, way).wait_send()
            h_first(block, way).wait_send()
            h_second(block, way).wait_send()
            r_far(block, way).wait_send()
            r_direct(block, way).wait_send()
            r_joined(block, way).wait_send()

    for one in w_first + w_second + w_across + [pair_copy, state_copy]:
        one.wait_send()


def body(
    sizes,
    layer_in,
    attn_gain,
    qkv_weight,
    log_decay,
    write_rate,
    head_gain,
    out_weight,
    ffn_gain,
    gate_weight,
    up_weight,
    down_weight,
):
    x_size, z_size, tp_size = sizes
    length, slice_width = layer_in.shape
    full = tp_size * slice_width
    width = head_gain.shape[0]
    heads = qkv_weight.shape[2] // width
    blocks = length // SPAN
    hidden = gate_weight.shape[1]
    shard_rows = out_weight.shape[0]

    def rows_of(per_token):
        return jnp.broadcast_to(
            per_token.reshape(heads * blocks, 1, SPAN), (heads * blocks, 8, SPAN)
        )

    vmem = pl.BlockSpec(memory_space=pltpu.VMEM)
    anywhere = pl.BlockSpec(memory_space=pl.ANY)
    dma = pltpu.SemaphoreType.DMA
    scratch = [
        pltpu.VMEM(qkv_weight.shape, BF16),
        pltpu.VMEM((tp_size * shard_rows, full), BF16),
        pltpu.VMEM(gate_weight.shape, BF16),
        pltpu.VMEM(up_weight.shape, BF16),
        pltpu.VMEM(down_weight.shape, BF16),
        pltpu.VMEM((tp_size, length, slice_width), BF16),
        pltpu.VMEM((tp_size, length, heads * width), BF16),
        pltpu.VMEM((heads, length, width), F32),
        pltpu.VMEM((heads, length, width), BF16),
        pltpu.VMEM((heads, width, 2 * width), F32),
        pltpu.VMEM((heads, 8, width), F32),
        pltpu.VMEM((heads, width + 16, 2 * width), BF16),
        pltpu.VMEM((heads, width + 16, 2 * width), BF16),
        pltpu.VMEM((z_size, width + 16, 2 * width), BF16),
        pltpu.VMEM((x_size, width + 16, 2 * width), BF16),
        pltpu.VMEM((width, 2 * width), F32),
        pltpu.VMEM((8, width), F32),
        pltpu.VMEM((heads, width, width), F32),
        pltpu.VMEM((blocks, tp_size, SPAN, slice_width), BF16),
        pltpu.VMEM((2, blocks, SPAN // 2, slice_width), BF16),
        pltpu.VMEM((2, blocks, SPAN // 2, slice_width), BF16),
        pltpu.VMEM((2, blocks, SPAN, slice_width), BF16),
        pltpu.VMEM((tp_size, SPAN, slice_width), F32),
        pltpu.VMEM((length, slice_width), F32),
        dma((5,)),
        dma((4, blocks)),
        dma((4, blocks)),
        dma((4, blocks)),
        dma((4, blocks)),
        dma((6, blocks)),
        dma((6, blocks)),
        dma((7,)),
        dma((7,)),
        dma((2,)),
        dma((2,)),
        dma((2, z_size)),
        dma((2, z_size)),
        dma((2, x_size)),
        dma((2, x_size)),
    ]
    return pl.pallas_call(
        functools.partial(layer_kernel, (x_size, z_size, tp_size, blocks)),
        out_shape=jax.ShapeDtypeStruct((length, slice_width), BF16),
        in_specs=[vmem] * 6 + [anywhere] * 5,
        out_specs=vmem,
        scratch_shapes=scratch,
        compiler_params=pltpu.CompilerParams(
            collective_id=0, has_side_effects=True, vmem_limit_bytes=60 * 1024 * 1024
        ),
        name="layer",
    )(
        layer_in,
        attn_gain.reshape(1, full),
        rows_of(log_decay),
        rows_of(write_rate),
        head_gain.reshape(1, width),
        ffn_gain.reshape(1, full),
        qkv_weight,
        out_weight,
        gate_weight,
        up_weight,
        down_weight,
    )


def layer(shape, tp_size):
    x_size, z_size, cores = shape
    in_specs = (
        P(SEQ, "tp"),
        P(),
        P(None, None, "tp"),
        P("tp", SEQ),
        P("tp", SEQ),
        P(),
        P("tp", None),
        P(),
        P(None, "tp"),
        P(None, "tp"),
        P("tp", None),
    )
    return functools.partial(body, (x_size, z_size, tp_size)), in_specs, P(SEQ, "tp")


def solution(mesh):
    torus = Mesh(mesh.devices.reshape(4, 8, 2, mesh.shape["tp"]), (*SEQ, "tp"))
    function, in_specs, out_specs = layer((4, 8, 2), mesh.shape["tp"])
    return jax.shard_map(
        function, mesh=torus, in_specs=in_specs, out_specs=out_specs, check_vma=False
    )
```

time: 482 us -> 125 us (0.26); the launches traced: 474 us -> 125 us
  blocking collectives: 153 us -> 0 us
  other arithmetic: 138 us -> 0 us
  Pallas kernels: 0 us -> 121 us
  waiting for transfers between devices: 86.5 us -> 0 us
  matrix products: 67.3 us -> 0 us
  between operations: 14.5 us -> 0.01 us
  starting transfers between devices: 4.93 us -> 0 us
  local copies, waits for them, and re-layouts: 9.61 us -> 4.71 us
    pallas_call x0 -> x1, Pallas kernels: none -> 121 us  [body(): pl.pallas_call(functools.partial(layer_kernel, (x_size, z_size, tp_size,...]
    another operation x6 -> x0, other arithmetic: 119 us -> none  [the longest x3 119 us: block_terms(): jax.scipy.linalg.solve_triangular(system, right_side, lower=True, unit_di...]
    all_gather x2 -> x0, waiting for transfers between devices: 82.9 us -> none  [the longest x1 43.3 us: body(): lax.all_gather(layer_in, 'tp', axis=1, tiled=True).astype(jnp.float32)]
    all_gather x6 -> x0, blocking collectives: 81 us -> none  [prefix_by_axis(): lax.all_gather(part.astype(kind), axis)]
    all_to_all x2 -> x0, blocking collectives: 72.2 us -> none  [summed_on_arrival(): lax.all_to_all(in_blocks(shard, dim, peers), axis, 0, 0, tiled=True)]
    dot_general x66 -> x0, matrix products: 65.8 us -> none  [the longest x29 17.9 us: compose(): jnp.einsum('hij,hjk->hik', second_map, first_shift, precision=highest)]
    dynamic_update_slice x12 -> x0, other arithmetic: 8.75 us -> none  [body(): lax.scan(advance, start, (transfer.transpose(1, 0, 2, 3), offset.transpos...]
  transfers between devices with their start and end apart: 3 -> 0, of which waited for: 3 -> 0; matrix products, arithmetic and copies ran while one was open for 1% -> 0% of each run, Pallas kernels for 0% -> 0%
where the time goes in v1:
time: 125 us
  Pallas kernels  121 us (97%)
  local copies, waits for them, and re-layouts  4.71 us (4%)
    pallas_call x1, Pallas kernels, body(): pl.pallas_call(functools.partial(layer_kernel, (x_size, z_size, tp_size,...  121 us
    broadcast_in_dim x4, local copies, waits for them, and re-layouts, rows_of(): jnp.broadcast_to(per_token.reshape(heads * blocks, 1, SPAN), (heads * blo...  2.64 us

profile of v1, /device:TPU:8, one launch (start us, length us, event | category | flops | bytes accessed | tf_op | source)
XLA Modules:
  0.0 125.3 jit_solution(13485626216000331536)
XLA Ops:
  0.0 0.7 broadcast_in_dim.14
  0.7 0.7 broadcast_in_dim.16
  1.4 0.6 broadcast_in_dim.17.rate_ref
  2.0 0.6 broadcast_in_dim.15.decay_ref
  2.6 120.6 %layer.1 = bf16[768,512]{1,0:T(8,128)(2,1)} custom-call(bf16[768,512]{1,0:T(8,128)(2,1)} %x_ref.1, f32[1,2048]{1,0:T(1,128)} %bitcast.3, f32[12,8,128]{2,1,0:T(8,128)} %broadcast_in_dim.15.decay_ref, f32[12,8,128]{2,1,0:T(8,128)} %broadcast_in_dim.17.rate_ref, f32[1,128]{1,0:T(1,128)} %bitcast.5, f32[1,2048]{1,0:T(1,128)} %bitcast.4, ...), custom_call_target="tpu_custom_call" | custom-call | tf_op jit(solution)/shard_map/layer/pallas_call | solution.py:649
  123.2 2.1 %copy.13 = bf16[768,512]{1,0:T(8,128)(2,1)} copy(bf16[768,512]{1,0:T(8,128)(2,1)} %layer.1) | data formatting | bytes 1572864

commit v2 on v1

v2 whole, which is shorter than its diff:
```python
import functools

import jax
import jax.numpy as jnp
from jax import lax
from jax.experimental import pallas as pl
from jax.experimental.pallas import tpu as pltpu
from jax.sharding import Mesh
from jax.sharding import PartitionSpec as P

SEQ = ("seq_0", "seq_1", "seq_2")
MESH = pl.DeviceIdType.MESH
BF16 = jnp.bfloat16
F32 = jnp.float32

norm_floor = 0.1
head_floor = 0.05
SPAN = 128
GROUP = 2
AHEAD = 2


def mm(a, b, dims=((1,), (0,))):
    return lax.dot_general(
        a.astype(BF16), b.astype(BF16), (dims, ((), ())), preferred_element_type=F32
    )


def mm_exact(a, b):
    return lax.dot_general(
        a, b, (((1,), (0,)), ((), ())), preferred_element_type=F32, precision=lax.Precision.HIGHEST
    )


def unit_rows(vectors):
    return vectors * lax.rsqrt(jnp.sum(vectors * vectors, axis=-1, keepdims=True) + 1.0)


def iotas(size):
    rows = lax.broadcasted_iota(jnp.int32, (size, size), 0)
    cols = lax.broadcasted_iota(jnp.int32, (size, size), 1)
    return (rows, cols)


def inverses(lowers):
    size = lowers[0].shape[0]
    rows, cols = iotas(size)
    pairs = rows // 2 == cols // 2
    found = [jnp.where(rows == cols, 1.0, jnp.where(pairs, -a, 0.0)) for a in lowers]
    block = 2
    while block < size:
        pick = (rows // (2 * block) == cols // (2 * block)) & (rows // block != cols // block)
        inner = [mm(jnp.where(pick, a, 0.0), x) for a, x in zip(lowers, found)]
        found = [x - mm(x, y) for x, y in zip(found, inner)]
        block *= 2
    return found


def compose(earlier, later):
    first_growth, first = earlier
    second_growth, second = later
    width = first.shape[0]
    second_map = second[:, :width]
    both_growth = jnp.concatenate([second_growth, second_growth], axis=1)
    own = jnp.concatenate([first_growth * second_map, second[:, width:]], axis=1)
    return (first_growth * second_growth, both_growth * first + own - mm(second_map, first))


def apply_terms(terms, state):
    growth, both = terms
    width = both.shape[0]
    return growth * state - mm(both[:, :width], state) + both[:, width:]


def packed(terms):
    growth, both = terms
    high = growth.astype(BF16).astype(F32)
    middle = (growth - high).astype(BF16).astype(F32)
    low = growth - high - middle
    width = both.shape[0]
    row = lax.broadcasted_iota(jnp.int32, (16, width), 0)
    parts = jnp.where(row == 0, high, jnp.where(row == 1, middle, jnp.where(row == 2, low, 0.0)))
    return jnp.concatenate([both[:, :width], parts], axis=0).astype(BF16), both[:, width:].astype(BF16)


def keep(message, terms):
    upper, lower = packed(terms)
    message[0] = upper
    message[1, pl.ds(0, lower.shape[0]), :] = lower


def unpacked(message):
    width = message.shape[2]
    upper = message[0].astype(F32)
    growth = upper[width : width + 1] + upper[width + 1 : width + 2] + upper[width + 2 : width + 3]
    lower = message[1, pl.ds(0, width), :].astype(F32)
    return (growth, jnp.concatenate([upper[:width], lower], axis=1))


def choose(first, terms, others):
    return tuple(jnp.where(first, a, b) for a, b in zip(terms, others))


def ring_gather(axis, size, held, send_sem, recv_sem, arrived):
    here = lax.axis_index(axis)
    right, left = (lax.rem(here + 1, size), lax.rem(here + size - 1, size))
    width = held.shape[3]

    def copy(way, step, part):
        owner = lax.rem(here + size - step, size) if way == 0 else lax.rem(here + step, size)
        piece = held.at[owner, part, pl.ds(0, width + 16 if part == 0 else width)]
        return pltpu.make_async_remote_copy(
            src_ref=piece,
            dst_ref=piece,
            send_sem=send_sem.at[way, part, step],
            recv_sem=recv_sem.at[way, part, step],
            device_id={axis: right if way == 0 else left},
            device_id_type=MESH,
        )

    steps = size // 2
    order = ((0, 1), (1, 0))
    copies = [
        [
            {
                part: copy(way, step, part)
                for part in order[way]
                if part == way or 2 * (step + 1) < size
            }
            for step in range(steps)
        ]
        for way in (0, 1)
    ]
    for n in (0, 1):
        for way in (0, 1):
            if order[way][n] in copies[way][0]:
                copies[way][0][order[way][n]].start()
    arrived(-1, ())
    for step in range(steps):
        for n in (0, 1):
            for way in (0, 1):
                part = order[way][n]
                if part in copies[way][step]:
                    copies[way][step][part].wait_recv()
                    if step + 1 < steps and part in copies[way][step + 1]:
                        copies[way][step + 1][part].start()
        arrived(step, (0, 1) if 2 * (step + 1) < size else (0,))
    return [one for way in copies for step in way for one in step.values()]


def layer_kernel(
    sizes,
    x_ref,
    attn_gain_ref,
    decay_ref,
    rate_ref,
    head_gain_ref,
    ffn_gain_ref,
    qkv_hbm,
    out_hbm,
    gate_hbm,
    up_hbm,
    down_hbm,
    o_ref,
    qkv_w,
    out_w,
    gate_w,
    up_w,
    down_w,
    rows_all,
    terms_all,
    running,
    growth_now,
    fade_of,
    system_of,
    grown_of,
    side_of,
    rate_of,
    tail_of,
    total_of,
    pair_mine,
    pair_other,
    z_held,
    x_held,
    states,
    leaving,
    parts,
    passing,
    joined,
    landed,
    resid,
    kept,
    load_sem,
    x_send,
    x_recv,
    h_send,
    h_recv,
    r_send,
    r_recv,
    w_send,
    w_recv,
    wz_send,
    wz_recv,
    wx_send,
    wx_recv,
    st_send,
    st_recv,
    pair_send,
    pair_recv,
    z_send,
    z_recv,
    s_send,
    s_recv,
):
    x_size, z_size, tp_size, blocks = sizes
    me = lax.axis_index("tp")
    core = lax.axis_index("seq_2")
    z_here = lax.axis_index("seq_1")
    x_here = lax.axis_index("seq_0")
    right, left = (lax.rem(me + 1, tp_size), lax.rem(me + tp_size - 1, tp_size))
    opposite = lax.rem(me + 2, tp_size)
    width = head_gain_ref.shape[1]
    heads = decay_ref.shape[0]
    slice_width = x_ref.shape[1]
    shard_rows = heads * width
    half = SPAN // 2
    near = {"tp": right}, {"tp": left}

    loads = [
        pltpu.make_async_copy(qkv_hbm, qkv_w, load_sem.at[0]),
        pltpu.make_async_copy(out_hbm, out_w.at[0], load_sem.at[1]),
        pltpu.make_async_copy(gate_hbm, gate_w, load_sem.at[2]),
        pltpu.make_async_copy(up_hbm, up_w, load_sem.at[3]),
        pltpu.make_async_copy(down_hbm, down_w, load_sem.at[4]),
    ]
    for load in loads:
        load.start()

    barrier = pltpu.get_barrier_semaphore()
    around = (right, left, opposite)
    friends = [{"tp": other} for other in around] + [{"seq_2": 1 - core}]
    friends += [{"tp": other, "seq_2": 1 - core} for other in around]
    for axis, here, size in (("seq_1", z_here, z_size), ("seq_0", x_here, x_size)):
        friends.append({axis: lax.rem(here + 1, size)})
        friends.append({axis: lax.rem(here + size - 1, size)})
    for friend in friends:
        pl.semaphore_signal(barrier, inc=1, device_id=friend, device_id_type=MESH)
    pl.semaphore_wait(barrier, len(friends))

    def span_of(block, start=0, size=SPAN):
        return pl.ds(pl.multiple_of(block * SPAN + start, half), size)

    def remote(source, target, send, recv, device):
        return pltpu.make_async_remote_copy(
            src_ref=source,
            dst_ref=target,
            send_sem=send,
            recv_sem=recv,
            device_id=device,
            device_id_type=MESH,
        )

    group = GROUP * SPAN
    groups = blocks // GROUP

    def group_of(block, start=0, size=group):
        return pl.ds(pl.multiple_of(block * group + start, half), size)

    def x_first(block, way):
        there = rows_all.at[me, group_of(block)]
        return remote(
            x_ref.at[group_of(block)], there, x_send.at[way, block], x_recv.at[way, block], near[way]
        )

    def x_second(block, way):
        owner = left if way == 0 else right
        there = rows_all.at[owner, group_of(block, way * group // 2, group // 2)]
        return remote(
            there, there, x_send.at[2 + way, block], x_recv.at[2 + way, block], near[way]
        )

    def t_first(block, way):
        there = terms_all.at[me, group_of(block)]
        return remote(there, there, h_send.at[way, block], h_recv.at[way, block], near[way])

    def t_second(block, way):
        owner = left if way == 0 else right
        there = terms_all.at[owner, group_of(block, way * group // 2, group // 2)]
        return remote(
            there, there, h_send.at[2 + way, block], h_recv.at[2 + way, block], near[way]
        )

    full = tp_size * slice_width
    core_rows = shard_rows // 2
    piece_rows = core_rows // z_size
    piece_cols = full // x_size

    def w_piece(z_at, x_at, start=0, size=piece_cols):
        first = pl.multiple_of(core * core_rows + z_at * piece_rows, piece_rows)
        return (
            pl.ds(first, piece_rows),
            pl.ds(pl.multiple_of(x_at * piece_cols + start, piece_cols // 2), size),
        )

    def w_column(x_at, start=0, size=piece_cols):
        return (
            pl.ds(pl.multiple_of(core * core_rows, core_rows), core_rows),
            pl.ds(pl.multiple_of(x_at * piece_cols + start, piece_cols // 2), size),
        )

    own_rows, own_cols = w_piece(z_here, x_here)
    w_cross = [
        remote(
            out_hbm.at[own_rows, own_cols],
            out_w.at[slot, own_rows, own_cols],
            w_send.at[n],
            w_recv.at[n],
            {"tp": other},
        )
        for n, (other, slot) in enumerate(zip(around, (2, 1, 3)))
    ]

    def w_ring(axis, here, size, region, send, recv):
        copies = []
        for step in range(size // 2):
            pair = []
            for way in (0, 1):
                owner = lax.rem(here + (size - step if way == 0 else step), size)
                last = 2 * (step + 1) == size
                half_cols = piece_cols // 2
                rows, cols = region(owner, way * half_cols, half_cols) if last else region(owner)
                there = out_w.at[pl.ds(1, tp_size - 1), rows, cols]
                onward = {axis: lax.rem(here + (1 if way == 0 else size - 1), size)}
                pair.append(remote(there, there, send.at[way, step], recv.at[way, step], onward))
            copies.append(pair)
        return copies

    w_z = w_ring(
        "seq_1", z_here, z_size, lambda at, *cut: w_piece(at, x_here, *cut), wz_send, wz_recv
    )
    w_x = w_ring("seq_0", x_here, x_size, w_column, wx_send, wx_recv)
    w_waves = [w_cross] + w_z + w_x
    half_out_w = out_w.at[pl.ds(1, tp_size - 1), pl.ds(pl.multiple_of(core * core_rows, core_rows), core_rows)]
    w_across = remote(half_out_w, half_out_w, w_send.at[3], w_recv.at[3], {"seq_2": 1 - core})

    def w_move(wave):
        for one in w_waves[wave]:
            one.wait_recv()
        for one in w_waves[wave + 1] if wave + 1 < len(w_waves) else [w_across]:
            one.start()

    def prepare(block):
        rows, cols = iotas(SPAN)
        ones = jnp.ones((SPAN, SPAN), F32)
        upper = jnp.where(rows <= cols, 1.0, 0.0)
        for h in range(heads):
            tokens = span_of(block)
            decay = jnp.broadcast_to(decay_ref[h : h + 1, tokens], (SPAN, SPAN))
            rate = jnp.broadcast_to(rate_ref[h : h + 1, tokens], (SPAN, SPAN))
            along = mm_exact(decay[0:8], upper)[0:1]
            total = mm_exact(decay[0:8], ones)[0:1]
            down = mm_exact(jnp.where(rows >= cols, decay, 0.0), ones)
            beta = mm_exact(jnp.where(rows == cols, rate, 0.0), ones)
            fade = jnp.where(rows >= cols, jnp.exp(jnp.minimum(down - along, 0.0)), 0.0)
            grown = jnp.exp(down)
            fade_of[h, tokens, :] = fade
            system_of[h, tokens, :] = jnp.where(rows > cols, beta * fade, 0.0)
            grown_of[h, tokens, :] = grown
            side_of[h, tokens, :] = beta * grown
            rate_of[h, tokens, :] = beta
            tail_of[h, tokens, :] = jnp.exp(total - down)
            total_of[h, block] = jnp.broadcast_to(jnp.exp(total), total_of.shape[2:])

    def project(block):
        tokens = group_of(block)
        spread = [rows_all[j, tokens, :].astype(F32) for j in range(tp_size)]
        squares = sum(jnp.sum(part * part, axis=1, keepdims=True) for part in spread)
        scale = lax.rsqrt(squares * (1.0 / (tp_size * slice_width)) + norm_floor)
        normed = jnp.concatenate(
            [
                (part * scale * attn_gain_ref[:, j * slice_width : (j + 1) * slice_width]).astype(
                    BF16
                )
                for j, part in enumerate(spread)
            ],
            axis=1,
        )
        return normed

    chains = [(c, h) for c in range(GROUP) for h in range(heads)]

    def cut(part):
        return [part[c * SPAN : (c + 1) * SPAN, h * width : (h + 1) * width] for c, h in chains]

    def recur(block):
        normed = project(block)
        spans = [span_of(block * GROUP + c) for c, h in chains]

        def stored(ref):
            return [ref[h, tokens, :] for (c, h), tokens in zip(chains, spans)]

        keys = [unit_rows(part) for part in cut(jnp.dot(normed, qkv_w[1], preferred_element_type=F32))]
        key_key = [mm(k, k, ((1,), (1,))) for k in keys]
        values = cut(jnp.dot(normed, qkv_w[2], preferred_element_type=F32))
        inverse = inverses([kk * f for kk, f in zip(key_key, stored(system_of))])
        sides = [
            jnp.concatenate([g * k, b * v], axis=1)
            for b, g, k, v in zip(stored(rate_of), stored(side_of), keys, values)
        ]
        solved = [mm(x, s).astype(BF16) for x, s in zip(inverse, sides)]
        tails = [k * t for k, t in zip(keys, stored(tail_of))]
        terms = [mm(k, s, ((0,), (0,))) for k, s in zip(tails, solved)]
        before = []
        for n, (c, h) in enumerate(chains):
            growth = growth_now[h][0:1]
            entry_terms = running[h]
            before.append((growth, entry_terms))
            step = total_of[h, block * GROUP + c][0:1]
            new_growth, new_terms = compose((growth, entry_terms), (step, terms[n]))
            running[h] = new_terms
            growth_now[h] = jnp.broadcast_to(new_growth, growth_now.shape[1:])
        return (block, spans, stored, normed, keys, solved, before)

    def query(known):
        block, spans, stored, normed, keys, solved, before = known
        queries = [unit_rows(part) for part in cut(jnp.dot(normed, qkv_w[0], preferred_element_type=F32))]
        query_key = [mm(q, k, ((1,), (1,))) for q, k in zip(queries, keys)]
        mixed = [mm(qk * f, s) for qk, f, s in zip(query_key, stored(fade_of), solved)]
        entries = [
            g * q - m[:, :width] for g, q, m in zip(stored(grown_of), queries, mixed)
        ]
        reached = [mm(e, b[1]) for e, b in zip(entries, before)]
        for n, ((c, h), tokens) in enumerate(zip(chains, spans)):
            local = mixed[n][:, width:] + reached[n][:, width:]
            onward = before[n][0] * entries[n] - reached[n][:, :width]
            terms_all[me, tokens, h * width : (h + 1) * width] = local.astype(BF16)
            terms_all[me, tokens, (heads + h) * width : (heads + h + 1) * width] = onward.astype(
                BF16
            )

    rows_all[me] = x_ref[...]
    running[...] = jnp.zeros_like(running)
    growth_now[...] = jnp.ones_like(growth_now)
    for one in w_cross:
        one.start()
    for block in range(min(AHEAD, groups)):
        for way in (0, 1):
            x_first(block, way).start()

    @pl.loop(0, blocks)
    def _(block):
        prepare(block)

    loads[0].wait()
    w_move(0)

    slots = [(n, when) for n in range(groups) for when in (("early", "late") if n else ("early",))]
    plan = list(zip(range(1, len(w_waves) - 2), slots))
    early = [(wave, n) for wave, (n, when) in plan if when == "early"]
    late = [(wave, n) for wave, (n, when) in plan if when == "late"]

    @pl.loop(0, groups)
    def _(block):
        for way in (0, 1):
            x_first(block, way).wait_recv()
            x_second(block, way).start()

        @pl.when(block + AHEAD < groups)
        def _():
            for way in (0, 1):
                x_first(block + AHEAD, way).start()

        for wave, at in early:

            @pl.when(block == at)
            def _(wave=wave):
                w_move(wave)

        @pl.when(block > 0)
        def _():
            for way in (0, 1):
                x_second(block - 1, way).wait_recv()
            query(recur(block - 1))

        for wave, at in late:

            @pl.when(block == at)
            def _(wave=wave):
                w_move(wave)

    for block in range(groups - 1):
        for way in (0, 1):
            t_first(block, way).start()
    for way in (0, 1):
        x_second(groups - 1, way).wait_recv()
    last = recur(groups - 1)
    w_left = len(w_waves) - 1 - len(early) - len(late)
    for wave in range(len(w_waves) - w_left, len(w_waves) - 1):
        w_move(wave)

    partner = {"seq_2": 1 - core}
    for h in range(heads):
        keep(pair_mine.at[h], (growth_now[h][0:1], running[h]))
    pair_copy = remote(pair_mine, pair_other, pair_send.at[0], pair_recv.at[0], partner)
    pair_copy.start()
    pair_copy.wait_recv()
    own, other = (unpacked(pair_mine.at[core]), unpacked(pair_other.at[core]))
    chip = compose(choose(core == 0, own, other), choose(core == 0, other, own))
    keep(z_held.at[z_here], chip)
    nothing = (jnp.ones((1, width), F32), jnp.zeros((width, 2 * width), F32))
    sums = {"before": [nothing, nothing], "after": [nothing, nothing]}

    def t_pass(block):
        for way in (0, 1):
            t_first(block, way).wait_recv()
            t_second(block, way).start()

    def z_arrived(step, ways):
        if step < 0:
            query(last)
            for way in (0, 1):
                t_first(groups - 1, way).start()
        if 0 < step < groups:
            t_pass(step - 1)
        for way in ways:
            earlier = z_here > step if way == 0 else z_here + 1 + step >= z_size
            owner = lax.rem(z_here + (z_size - 1 - step if way == 0 else 1 + step), z_size)
            item = unpacked(z_held.at[owner])
            so_far = choose(earlier, sums["before"][way], sums["after"][way])
            joint = compose(item, so_far) if way == 0 else compose(so_far, item)
            sums["before"][way] = choose(earlier, joint, sums["before"][way])
            sums["after"][way] = choose(earlier, sums["after"][way], joint)

    ring_copies = ring_gather("seq_1", z_size, z_held, z_send, z_recv, z_arrived)
    through = compose(sums["before"][1], sums["before"][0])
    rest = compose(sums["after"][1], sums["after"][0])
    keep(x_held.at[x_here], compose(compose(through, chip), rest))

    def x_arrived(step, ways):
        if step < 0:
            w_move(len(w_waves) - 1)
            for block in range(max(0, min(groups, z_size // 2) - 1), groups - 1):
                t_pass(block)
        if step == 0:
            t_pass(groups - 1)

    ring_copies += ring_gather("seq_0", x_size, x_held, s_send, s_recv, x_arrived)
    chosen = jnp.zeros((width, width), F32)
    for back in range(x_size - 1, 0, -1):
        owner = lax.rem(x_here + x_size - back, x_size)
        chosen = jnp.where(x_here >= back, apply_terms(unpacked(x_held.at[owner]), chosen), chosen)
    first_terms = choose(core == 0, own, other)
    reached = apply_terms(through, chosen)
    leaving[0] = reached.astype(BF16)
    leaving[1] = apply_terms(first_terms, reached).astype(BF16)
    states[me, core] = leaving[core]
    state_copies = []
    for n, device in enumerate(friends[:7]):
        there = core if n < 3 else 1 - core
        state_copies.append(
            remote(leaving.at[there], states.at[me, core], st_send.at[n], st_recv.at[n], device)
        )
    for n in (2, 6, 0, 1, 3, 4, 5):
        state_copies[n].start()
    for load in loads[1:]:
        load.wait()
    w_across.wait_recv()
    for block in range(groups):
        for way in (0, 1):
            t_second(block, way).wait_recv()
    for n, (origin, head) in enumerate(
        [(left, core), (right, core), (opposite, core)]
        + [(me, 1 - core)]
        + [(left, 1 - core), (right, 1 - core), (opposite, 1 - core)]
    ):
        remote(
            leaving.at[0], states.at[origin, head], st_send.at[n], st_recv.at[n], {"tp": right}
        ).wait_recv()

    def r_far(block, way):
        return remote(
            parts.at[block, opposite, pl.ds(way * half, half)],
            passing.at[way, block],
            r_send.at[way, block],
            r_recv.at[way, block],
            near[way],
        )

    def r_direct(block, way):
        target = right if way == 0 else left
        piece = pl.ds((1 - way) * half, half)
        return remote(
            parts.at[block, target, piece],
            landed.at[way, block, piece],
            r_send.at[2 + way, block],
            r_recv.at[2 + way, block],
            near[way],
        )

    def r_joined(block, way):
        return remote(
            joined.at[way, block],
            landed.at[way, block, pl.ds(way * half, half)],
            r_send.at[4 + way, block],
            r_recv.at[4 + way, block],
            near[way],
        )

    def feed_forward(block):
        outs = []
        for origin in (me, *around):
            for h in range(heads):
                local = terms_all[origin, span_of(block), h * width : (h + 1) * width]
                onward = terms_all[
                    origin, span_of(block), (heads + h) * width : (heads + h + 1) * width
                ]
                raw = local.astype(F32) + mm(onward, states[origin, h])
                level = jnp.mean(raw * raw, axis=-1, keepdims=True)
                outs.append((raw * lax.rsqrt(level + head_floor) * head_gain_ref[...]).astype(BF16))
        attended = jnp.concatenate(outs, axis=1)
        squares = jnp.zeros((SPAN, 1), F32)
        for j in range(tp_size):
            piece = rows_all[j, span_of(block), :].astype(F32) + jnp.dot(
                attended,
                out_w[:, :, j * slice_width : (j + 1) * slice_width].reshape(
                    tp_size * shard_rows, slice_width
                ),
                preferred_element_type=F32,
            )
            resid[j] = piece
            squares = squares + jnp.sum(piece * piece, axis=1, keepdims=True)
        scale = lax.rsqrt(squares * (1.0 / (tp_size * slice_width)) + norm_floor)
        normed = jnp.concatenate(
            [
                (
                    resid[j] * scale * ffn_gain_ref[:, j * slice_width : (j + 1) * slice_width]
                ).astype(BF16)
                for j in range(tp_size)
            ],
            axis=1,
        )
        kept[span_of(block), :] = resid[me]
        gate_act = jnp.dot(normed, gate_w[...], preferred_element_type=F32)
        up_act = jnp.dot(normed, up_w[...], preferred_element_type=F32)
        hidden = (jax.nn.silu(gate_act) * up_act).astype(BF16)
        for j in range(tp_size):
            parts[block, j] = jnp.dot(
                hidden,
                down_w[:, j * slice_width : (j + 1) * slice_width],
                preferred_element_type=F32,
            ).astype(BF16)

    def join(block):
        for way in (0, 1):
            r_far(block, way).wait_recv()
            target = right if way == 0 else left
            joined[way, block] = (
                passing[way, block].astype(F32)
                + parts[block, target, pl.ds(way * half, half), :].astype(F32)
            ).astype(BF16)
            r_joined(block, way).start()

    def finish(block):
        for way in (0, 1):
            r_direct(block, way).wait_recv()
            r_joined(block, way).wait_recv()
        total = kept[span_of(block), :] + parts[block, me].astype(F32)
        total = total + landed[0, block].astype(F32) + landed[1, block].astype(F32)
        o_ref[span_of(block), :] = total.astype(BF16)

    @pl.loop(0, blocks + 2)
    def _(block):
        @pl.when((block > 0) & (block < blocks + 1))
        def _():
            join(block - 1)

        @pl.when(block < blocks)
        def _():
            feed_forward(block)
            for way in (0, 1):
                r_far(block, way).start()
                r_direct(block, way).start()

        @pl.when(block > 1)
        def _():
            finish(block - 2)

    @pl.loop(0, blocks)
    def _(block):
        for way in (0, 1):
            r_far(block, way).wait_send()
            r_direct(block, way).wait_send()
            r_joined(block, way).wait_send()

    @pl.loop(0, groups)
    def _(block):
        for way in (0, 1):
            x_first(block, way).wait_send()
            x_second(block, way).wait_send()
            t_first(block, way).wait_send()
            t_second(block, way).wait_send()

    w_copies = [one for wave in w_waves for one in wave] + [w_across]
    for one in w_copies + state_copies + [pair_copy] + ring_copies:
        one.wait_send()


def body(
    sizes,
    layer_in,
    attn_gain,
    qkv_weight,
    log_decay,
    write_rate,
    head_gain,
    out_weight,
    ffn_gain,
    gate_weight,
    up_weight,
    down_weight,
):
    x_size, z_size, tp_size = sizes
    length, slice_width = layer_in.shape
    full = tp_size * slice_width
    width = head_gain.shape[0]
    heads = qkv_weight.shape[2] // width
    blocks = length // SPAN
    hidden = gate_weight.shape[1]
    shard_rows = out_weight.shape[0]

    vmem = pl.BlockSpec(memory_space=pltpu.VMEM)
    anywhere = pl.BlockSpec(memory_space=pl.ANY)
    dma = pltpu.SemaphoreType.DMA
    scratch = [
        pltpu.VMEM(qkv_weight.shape, BF16),
        pltpu.VMEM((tp_size, shard_rows, full), BF16),
        pltpu.VMEM(gate_weight.shape, BF16),
        pltpu.VMEM(up_weight.shape, BF16),
        pltpu.VMEM(down_weight.shape, BF16),
        pltpu.VMEM((tp_size, length, slice_width), BF16),
        pltpu.VMEM((tp_size, length, 2 * heads * width), BF16),
        pltpu.VMEM((heads, width, 2 * width), F32),
        pltpu.VMEM((heads, 8, width), F32),
        *[pltpu.VMEM((heads, length, SPAN), F32) for _ in range(6)],
        pltpu.VMEM((heads, blocks, 8, width), F32),
        pltpu.VMEM((heads, 2, width + 16, width), BF16),
        pltpu.VMEM((heads, 2, width + 16, width), BF16),
        pltpu.VMEM((z_size, 2, width + 16, width), BF16),
        pltpu.VMEM((x_size, 2, width + 16, width), BF16),
        pltpu.VMEM((tp_size, heads, width, width), BF16),
        pltpu.VMEM((2, width, width), BF16),
        pltpu.VMEM((blocks, tp_size, SPAN, slice_width), BF16),
        pltpu.VMEM((2, blocks, SPAN // 2, slice_width), BF16),
        pltpu.VMEM((2, blocks, SPAN // 2, slice_width), BF16),
        pltpu.VMEM((2, blocks, SPAN, slice_width), BF16),
        pltpu.VMEM((tp_size, SPAN, slice_width), F32),
        pltpu.VMEM((length, slice_width), F32),
        dma((5,)),
        dma((4, blocks // GROUP)),
        dma((4, blocks // GROUP)),
        dma((4, blocks // GROUP)),
        dma((4, blocks // GROUP)),
        dma((6, blocks)),
        dma((6, blocks)),
        dma((4,)),
        dma((4,)),
        dma((2, z_size // 2)),
        dma((2, z_size // 2)),
        dma((2, x_size // 2)),
        dma((2, x_size // 2)),
        dma((7,)),
        dma((7,)),
        dma((2,)),
        dma((2,)),
        dma((2, 2, z_size)),
        dma((2, 2, z_size)),
        dma((2, 2, x_size)),
        dma((2, 2, x_size)),
    ]
    return pl.pallas_call(
        functools.partial(layer_kernel, (x_size, z_size, tp_size, blocks)),
        out_shape=jax.ShapeDtypeStruct((length, slice_width), BF16),
        in_specs=[vmem] * 6 + [anywhere] * 5,
        out_specs=vmem,
        scratch_shapes=scratch,
        compiler_params=pltpu.CompilerParams(
            collective_id=0, has_side_effects=True, vmem_limit_bytes=60 * 1024 * 1024
        ),
        name="layer",
    )(
        layer_in,
        attn_gain.reshape(1, full),
        log_decay,
        write_rate,
        head_gain.reshape(1, width),
        ffn_gain.reshape(1, full),
        qkv_weight,
        out_weight,
        gate_weight,
        up_weight,
        down_weight,
    )


def layer(shape, tp_size):
    x_size, z_size, cores = shape
    in_specs = (
        P(SEQ, "tp"),
        P(),
        P(None, None, "tp"),
        P("tp", SEQ),
        P("tp", SEQ),
        P(),
        P("tp", None),
        P(),
        P(None, "tp"),
        P(None, "tp"),
        P("tp", None),
    )
    return functools.partial(body, (x_size, z_size, tp_size)), in_specs, P(SEQ, "tp")


def solution(mesh):
    torus = Mesh(mesh.devices.reshape(4, 8, 2, mesh.shape["tp"]), (*SEQ, "tp"))
    function, in_specs, out_specs = layer((4, 8, 2), mesh.shape["tp"])
    return jax.shard_map(
        function, mesh=torus, in_specs=in_specs, out_specs=out_specs, check_vma=False
    )
```

time: 125 us -> 118 us (0.944)
  Pallas kernels: 121 us -> 116 us
  local copies, waits for them, and re-layouts: 4.71 us -> 2.06 us
    pallas_call x1, Pallas kernels: 121 us -> 116 us  [body(): pl.pallas_call(functools.partial(layer_kernel, (x_size, z_size, tp_size,...]
    broadcast_in_dim x4 -> x0, local copies, waits for them, and re-layouts: 2.64 us -> none  [rows_of(): jnp.broadcast_to(per_token.reshape(heads * blocks, 1, SPAN), (heads * blo...]
where the time goes in v2:
time: 118 us
  Pallas kernels  116 us (98%)
  local copies, waits for them, and re-layouts  2.06 us (2%)
    pallas_call x1, Pallas kernels, body(): pl.pallas_call(functools.partial(layer_kernel, (x_size, z_size, tp_size,...  116 us

profile of v2, /device:TPU:8, one launch (start us, length us, event | category | flops | bytes accessed | tf_op | source)
XLA Modules:
  0.0 117.6 jit_solution(12404851581585667214)
XLA Ops:
  0.0 115.5 %layer.1 = bf16[768,512]{1,0:T(8,128)(2,1)} custom-call(bf16[768,512]{1,0:T(8,128)(2,1)} %x_ref.1, f32[1,2048]{1,0:T(1,128)} %bitcast.3, f32[2,768]{1,0:T(2,128)} %decay_ref.1, f32[2,768]{1,0:T(2,128)} %rate_ref.1, f32[1,128]{1,0:T(1,128)} %bitcast.5, f32[1,2048]{1,0:T(1,128)} %bitcast.4, bf16[3,2048,256]{2,1,0:T(8,128)(2,1)} %qkv_hbm.1, ...), custom_call_target="tpu_custom_call" | custom-call | tf_op jit(solution)/shard_map/layer/pallas_call | solution.py:780
  115.5 2.1 %copy.13 = bf16[768,512]{1,0:T(8,128)(2,1)} copy(bf16[768,512]{1,0:T(8,128)(2,1)} %layer.1) | data formatting | bytes 1572864

commit v3 on v2

--- a/solution.py
+++ b/solution.py
@@ -17,7 +17,7 @@
 head_floor = 0.05
 SPAN = 128
 GROUP = 2
-AHEAD = 2
+AHEAD = 3
 
 
 def mm(a, b, dims=((1,), (0,))):
@@ -49,10 +49,13 @@
     found = [jnp.where(rows == cols, 1.0, jnp.where(pairs, -a, 0.0)) for a in lowers]
     block = 2
     while block < size:
-        pick = (rows // (2 * block) == cols // (2 * block)) & (rows // block != cols // block)
-        inner = [mm(jnp.where(pick, a, 0.0), x) for a, x in zip(lowers, found)]
-        found = [x - mm(x, y) for x, y in zip(found, inner)]
-        block *= 2
+        wide = min(4 * block, size)
+        pick = (rows // wide == cols // wide) & (rows // block != cols // block)
+        inner = [mm(x, jnp.where(pick, a, 0.0)) for a, x in zip(lowers, found)]
+        near = [x - mm(n, x) for n, x in zip(inner, found)]
+        twice = [mm(n, n) for n in inner]
+        found = [x + mm(n, x) for n, x in zip(twice, near)]
+        block *= 4
     return found
 
 
@@ -233,9 +236,6 @@
         pltpu.make_async_copy(up_hbm, up_w, load_sem.at[3]),
         pltpu.make_async_copy(down_hbm, down_w, load_sem.at[4]),
     ]
-    for load in loads:
-        load.start()
-
     barrier = pltpu.get_barrier_semaphore()
     around = (right, left, opposite)
     friends = [{"tp": other} for other in around] + [{"seq_2": 1 - core}]
@@ -245,6 +245,8 @@
         friends.append({axis: lax.rem(here + size - 1, size)})
     for friend in friends:
         pl.semaphore_signal(barrier, inc=1, device_id=friend, device_id_type=MESH)
+    for load in loads:
+        load.start()
     pl.semaphore_wait(barrier, len(friends))
 
     def span_of(block, start=0, size=SPAN):
@@ -267,14 +269,14 @@
         return pl.ds(pl.multiple_of(block * group + start, half), size)
 
     def x_first(block, way):
-        there = rows_all.at[me, group_of(block)]
+        there = rows_all.at[me, span_of(block)]
         return remote(
-            x_ref.at[group_of(block)], there, x_send.at[way, block], x_recv.at[way, block], near[way]
+            x_ref.at[span_of(block)], there, x_send.at[way, block], x_recv.at[way, block], near[way]
         )
 
     def x_second(block, way):
         owner = left if way == 0 else right
-        there = rows_all.at[owner, group_of(block, way * group // 2, group // 2)]
+        there = rows_all.at[owner, span_of(block, way * half, half)]
         return remote(
             there, there, x_send.at[2 + way, block], x_recv.at[2 + way, block], near[way]
         )
@@ -438,14 +440,15 @@
                 BF16
             )
 
+    for block in range(min(AHEAD, blocks)):
+        for way in (0, 1):
+            x_first(block, way).start()
+        if block == 0:
+            for one in w_cross:
+                one.start()
     rows_all[me] = x_ref[...]
     running[...] = jnp.zeros_like(running)
     growth_now[...] = jnp.ones_like(growth_now)
-    for one in w_cross:
-        one.start()
-    for block in range(min(AHEAD, groups)):
-        for way in (0, 1):
-            x_first(block, way).start()
 
     @pl.loop(0, blocks)
     def _(block):
@@ -461,14 +464,16 @@
 
     @pl.loop(0, groups)
     def _(block):
-        for way in (0, 1):
-            x_first(block, way).wait_recv()
-            x_second(block, way).start()
-
-        @pl.when(block + AHEAD < groups)
-        def _():
+        for part in range(GROUP):
+            now = block * GROUP + part
             for way in (0, 1):
-                x_first(block + AHEAD, way).start()
+                x_first(now, way).wait_recv()
+                x_second(now, way).start()
+
+            @pl.when(now + AHEAD < blocks)
+            def _(now=now):
+                for way in (0, 1):
+                    x_first(now + AHEAD, way).start()
 
         for wave, at in early:
 
@@ -478,8 +483,9 @@
 
         @pl.when(block > 0)
         def _():
-            for way in (0, 1):
-                x_second(block - 1, way).wait_recv()
+            for part in range(GROUP):
+                for way in (0, 1):
+                    x_second((block - 1) * GROUP + part, way).wait_recv()
             query(recur(block - 1))
 
         for wave, at in late:
@@ -491,8 +497,9 @@
     for block in range(groups - 1):
         for way in (0, 1):
             t_first(block, way).start()
-    for way in (0, 1):
-        x_second(groups - 1, way).wait_recv()
+    for block in range(blocks - GROUP, blocks):
+        for way in (0, 1):
+            x_second(block, way).wait_recv()
     last = recur(groups - 1)
     w_left = len(w_waves) - 1 - len(early) - len(late)
     for wave in range(len(w_waves) - w_left, len(w_waves) - 1):
@@ -670,10 +677,6 @@
 
     @pl.loop(0, blocks + 2)
     def _(block):
-        @pl.when((block > 0) & (block < blocks + 1))
-        def _():
-            join(block - 1)
-
         @pl.when(block < blocks)
         def _():
             feed_forward(block)
@@ -681,6 +684,10 @@
                 r_far(block, way).start()
                 r_direct(block, way).start()
 
+        @pl.when((block > 0) & (block < blocks + 1))
+        def _():
+            join(block - 1)
+
         @pl.when(block > 1)
         def _():
             finish(block - 2)
@@ -688,6 +695,8 @@
     @pl.loop(0, blocks)
     def _(block):
         for way in (0, 1):
+            x_first(block, way).wait_send()
+            x_second(block, way).wait_send()
             r_far(block, way).wait_send()
             r_direct(block, way).wait_send()
             r_joined(block, way).wait_send()
@@ -695,8 +704,6 @@
     @pl.loop(0, groups)
     def _(block):
         for way in (0, 1):
-            x_first(block, way).wait_send()
-            x_second(block, way).wait_send()
             t_first(block, way).wait_send()
             t_second(block, way).wait_send()
 
@@ -756,8 +763,8 @@
         pltpu.VMEM((tp_size, SPAN, slice_width), F32),
         pltpu.VMEM((length, slice_width), F32),
         dma((5,)),
-        dma((4, blocks // GROUP)),
-        dma((4, blocks // GROUP)),
+        dma((4, blocks)),
+        dma((4, blocks)),
         dma((4, blocks // GROUP)),
         dma((4, blocks // GROUP)),
         dma((6, blocks)),

time: 118 us -> 106 us (0.90)
  Pallas kernels: 116 us -> 104 us
    pallas_call x1, Pallas kernels: 116 us -> 104 us  [body(): pl.pallas_call(functools.partial(layer_kernel, (x_size, z_size, tp_size,...]
where the time goes in v3:
time: 106 us
  Pallas kernels  104 us (98%)
  local copies, waits for them, and re-layouts  2.06 us (2%)
    pallas_call x1, Pallas kernels, body(): pl.pallas_call(functools.partial(layer_kernel, (x_size, z_size, tp_size,...  104 us

profile of v3, /device:TPU:8, one launch (start us, length us, event | category | flops | bytes accessed | tf_op | source)
XLA Modules:
  0.0 106.1 jit_solution(8928041780888934092)
XLA Ops:
  0.0 104.0 %layer.1 = bf16[768,512]{1,0:T(8,128)(2,1)} custom-call(bf16[768,512]{1,0:T(8,128)(2,1)} %x_ref.1, f32[1,2048]{1,0:T(1,128)} %bitcast.3, f32[2,768]{1,0:T(2,128)} %decay_ref.1, f32[2,768]{1,0:T(2,128)} %rate_ref.1, f32[1,128]{1,0:T(1,128)} %bitcast.5, f32[1,2048]{1,0:T(1,128)} %bitcast.4, bf16[3,2048,256]{2,1,0:T(8,128)(2,1)} %qkv_hbm.1, ...), custom_call_target="tpu_custom_call" | custom-call | tf_op jit(solution)/shard_map/layer/pallas_call | solution.py:787
  104.0 2.1 %copy.13 = bf16[768,512]{1,0:T(8,128)(2,1)} copy(bf16[768,512]{1,0:T(8,128)(2,1)} %layer.1) | data formatting | bytes 1572864

commit v4 on v3

--- a/solution.py
+++ b/solution.py
@@ -153,18 +153,23 @@
 
 def layer_kernel(
     sizes,
-    x_ref,
-    attn_gain_ref,
-    decay_ref,
-    rate_ref,
-    head_gain_ref,
-    ffn_gain_ref,
+    x_hbm,
+    attn_gain_hbm,
+    decay_hbm,
+    rate_hbm,
+    head_gain_hbm,
+    ffn_gain_hbm,
     qkv_hbm,
     out_hbm,
     gate_hbm,
     up_hbm,
     down_hbm,
     o_ref,
+    attn_gain_ref,
+    decay_ref,
+    rate_ref,
+    head_gain_ref,
+    ffn_gain_ref,
     qkv_w,
     out_w,
     gate_w,
@@ -224,7 +229,7 @@
     opposite = lax.rem(me + 2, tp_size)
     width = head_gain_ref.shape[1]
     heads = decay_ref.shape[0]
-    slice_width = x_ref.shape[1]
+    slice_width = x_hbm.shape[1]
     shard_rows = heads * width
     half = SPAN // 2
     near = {"tp": right}, {"tp": left}
@@ -236,6 +241,21 @@
         pltpu.make_async_copy(up_hbm, up_w, load_sem.at[3]),
         pltpu.make_async_copy(down_hbm, down_w, load_sem.at[4]),
     ]
+    early_loads = [
+        pltpu.make_async_copy(source, target, load_sem.at[5 + n])
+        for n, (source, target) in enumerate(
+            (
+                (x_hbm, rows_all.at[me]),
+                (decay_hbm, decay_ref),
+                (rate_hbm, rate_ref),
+                (attn_gain_hbm, attn_gain_ref),
+                (head_gain_hbm, head_gain_ref),
+                (ffn_gain_hbm, ffn_gain_ref),
+            )
+        )
+    ]
+    for load in early_loads:
+        load.start()
     barrier = pltpu.get_barrier_semaphore()
     around = (right, left, opposite)
     friends = [{"tp": other} for other in around] + [{"seq_2": 1 - core}]
@@ -247,6 +267,7 @@
         pl.semaphore_signal(barrier, inc=1, device_id=friend, device_id_type=MESH)
     for load in loads:
         load.start()
+    early_loads[0].wait()
     pl.semaphore_wait(barrier, len(friends))
 
     def span_of(block, start=0, size=SPAN):
@@ -270,9 +291,7 @@
 
     def x_first(block, way):
         there = rows_all.at[me, span_of(block)]
-        return remote(
-            x_ref.at[span_of(block)], there, x_send.at[way, block], x_recv.at[way, block], near[way]
-        )
+        return remote(there, there, x_send.at[way, block], x_recv.at[way, block], near[way])
 
     def x_second(block, way):
         owner = left if way == 0 else right
@@ -446,9 +465,11 @@
         if block == 0:
             for one in w_cross:
                 one.start()
-    rows_all[me] = x_ref[...]
     running[...] = jnp.zeros_like(running)
     growth_now[...] = jnp.ones_like(growth_now)
+
+    for load in early_loads[1:]:
+        load.wait()
 
     @pl.loop(0, blocks)
     def _(block):
@@ -739,6 +760,11 @@
     anywhere = pl.BlockSpec(memory_space=pl.ANY)
     dma = pltpu.SemaphoreType.DMA
     scratch = [
+        pltpu.VMEM((1, full), F32),
+        pltpu.VMEM((heads, length), F32),
+        pltpu.VMEM((heads, length), F32),
+        pltpu.VMEM((1, width), F32),
+        pltpu.VMEM((1, full), F32),
         pltpu.VMEM(qkv_weight.shape, BF16),
         pltpu.VMEM((tp_size, shard_rows, full), BF16),
         pltpu.VMEM(gate_weight.shape, BF16),
@@ -762,7 +788,7 @@
         pltpu.VMEM((2, blocks, SPAN, slice_width), BF16),
         pltpu.VMEM((tp_size, SPAN, slice_width), F32),
         pltpu.VMEM((length, slice_width), F32),
-        dma((5,)),
+        dma((11,)),
         dma((4, blocks)),
         dma((4, blocks)),
         dma((4, blocks // GROUP)),
@@ -786,8 +812,8 @@
     ]
     return pl.pallas_call(
         functools.partial(layer_kernel, (x_size, z_size, tp_size, blocks)),
-        out_shape=jax.ShapeDtypeStruct((length, slice_width), BF16),
-        in_specs=[vmem] * 6 + [anywhere] * 5,
+        out_shape=pltpu.VMEM((length, slice_width), BF16),
+        in_specs=[anywhere] * 11,
         out_specs=vmem,
         scratch_shapes=scratch,
         compiler_params=pltpu.CompilerParams(

time: 106 us -> 103 us (0.972)
  Pallas kernels: 104 us -> 102 us
  local copies, waits for them, and re-layouts: 2.06 us -> 0.88 us
    pallas_call x1, Pallas kernels: 104 us -> 102 us  [body(): pl.pallas_call(functools.partial(layer_kernel, (x_size, z_size, tp_size,...]
    unnamed x1, local copies, waits for them, and re-layouts: 2.06 us -> 0.88 us
where the time goes in v4:
time: 103 us
  Pallas kernels  102 us (99%)
    pallas_call x1, Pallas kernels, body(): pl.pallas_call(functools.partial(layer_kernel, (x_size, z_size, tp_size,...  102 us

profile of v4, /device:TPU:8, one launch (start us, length us, event | category | flops | bytes accessed | tf_op | source)
XLA Modules:
  0.0 102.9 jit_solution(10562556620244760585)
XLA Ops:
  0.0 102.0 %layer.1 = bf16[768,512]{1,0:T(8,128)(2,1)S(1)} custom-call(bf16[768,512]{1,0:T(8,128)(2,1)} %x_hbm.1, f32[1,2048]{1,0:T(1,128)} %bitcast.3, f32[2,768]{1,0:T(2,128)} %decay_hbm.1, f32[2,768]{1,0:T(2,128)} %rate_hbm.1, f32[1,128]{1,0:T(1,128)} %bitcast.5, f32[1,2048]{1,0:T(1,128)} %bitcast.4, bf16[3,2048,256]{2,1,0:T(8,128)(2,1)} %qkv_hbm.1, ...), custom_call_target="tpu_custom_call" | custom-call | tf_op jit(solution)/shard_map/layer/pallas_call | solution.py:813
  102.0 0.9 copy.13

commit v5 on v4

--- a/solution.py
+++ b/solution.py
@@ -564,6 +564,9 @@
     rest = compose(sums["after"][1], sums["after"][0])
     keep(x_held.at[x_here], compose(compose(through, chip), rest))
 
+    folded = []
+    first_terms = choose(core == 0, own, other)
+
     def x_arrived(step, ways):
         if step < 0:
             w_move(len(w_waves) - 1)
@@ -571,16 +574,25 @@
                 t_pass(block)
         if step == 0:
             t_pass(groups - 1)
+        if step == x_size // 2 - 2:
+            older, newer = (jnp.zeros((width, width), F32), nothing)
+            for back in range(x_size - 1, 0, -1):
+                item = unpacked(x_held.at[lax.rem(x_here + x_size - back, x_size)])
+                if back > x_size // 2:
+                    older = jnp.where(x_here >= back, apply_terms(item, older), older)
+                if back < x_size // 2:
+                    newer = choose(x_here >= back, compose(newer, item), newer)
+            folded.append((older, compose(newer, through)))
+            folded.append(compose(folded[0][1], first_terms))
 
     ring_copies += ring_gather("seq_0", x_size, x_held, s_send, s_recv, x_arrived)
-    chosen = jnp.zeros((width, width), F32)
-    for back in range(x_size - 1, 0, -1):
-        owner = lax.rem(x_here + x_size - back, x_size)
-        chosen = jnp.where(x_here >= back, apply_terms(unpacked(x_held.at[owner]), chosen), chosen)
-    first_terms = choose(core == 0, own, other)
-    reached = apply_terms(through, chosen)
-    leaving[0] = reached.astype(BF16)
-    leaving[1] = apply_terms(first_terms, reached).astype(BF16)
+    (chosen, to_first), to_second = folded
+    far = lax.rem(x_here + x_size - x_size // 2, x_size)
+    chosen = jnp.where(
+        x_here >= x_size // 2, apply_terms(unpacked(x_held.at[far]), chosen), chosen
+    )
+    leaving[0] = apply_terms(to_first, chosen).astype(BF16)
+    leaving[1] = apply_terms(to_second, chosen).astype(BF16)
     states[me, core] = leaving[core]
     state_copies = []
     for n, device in enumerate(friends[:7]):

time: 103 us -> 103 us (level)
  no operation moved by 1% of the time
where the time goes in v5:
time: 103 us; the launch traced here: 102 us
  Pallas kernels  102 us (99%)
    pallas_call x1, Pallas kernels, body(): pl.pallas_call(functools.partial(layer_kernel, (x_size, z_size, tp_size,...  102 us

profile of v5, /device:TPU:8, one launch (start us, length us, event | category | flops | bytes accessed | tf_op | source)
XLA Modules:
  0.0 102.5 jit_solution(3702193355930083077)
XLA Ops:
  0.0 101.6 %layer.1 = bf16[768,512]{1,0:T(8,128)(2,1)S(1)} custom-call(bf16[768,512]{1,0:T(8,128)(2,1)} %x_hbm.1, f32[1,2048]{1,0:T(1,128)} %bitcast.3, f32[2,768]{1,0:T(2,128)} %decay_hbm.1, f32[2,768]{1,0:T(2,128)} %rate_hbm.1, f32[1,128]{1,0:T(1,128)} %bitcast.5, f32[1,2048]{1,0:T(1,128)} %bitcast.4, bf16[3,2048,256]{2,1,0:T(8,128)(2,1)} %qkv_hbm.1, ...), custom_call_target="tpu_custom_call" | custom-call | tf_op jit(solution)/shard_map/layer/pallas_call | solution.py:825
  101.6 0.9 copy.13
